TPU v7x, 32 devices: a whole 2x2x4 slice. The times are simulated.
32 devices in a mesh: row: 4 (over z), col: 8 (over y, x, core).
Axes of the slice: x: 2, y: 2, z: 4, core: 2. Of those that a mesh axis runs over, the one named last changes fastest.
Arguments:
- tokens: bfloat16 [24576, 256], P(('row', 'col'))
- codebook: bfloat16 [16384, 256], P(('row', 'col')), may hold values from -6 to 6
- codes: int32 [24576], P(('row', 'col')), may hold values from 0 to 16383
Outputs:
- quantized: bfloat16 [24576, 256], P(('row', 'col'))
- token_loss: float32 [24576], P(('row', 'col'))
- code_counts: int32 [16384], P(('row', 'col'))
- code_loss: float32 [16384], P(('row', 'col'))
- commitment: float32 [], replicated
- perplexity: float32 [], replicated
All inputs are finite; a program needn't handle non-finite values.
Results may differ from a plain program's by a relative error of at most 0.0004.
Values may be sent and summed in bfloat16 or wider, within the bound.
No kernel may reach another device: no remote copies, remote signals or barrier semaphores. Data moves between devices by JAX's collectives and lax.ppermute only.
A program may use at most 64 MiB of HBM per device.

v0:
```python
import jax
import jax.numpy as jnp
from jax import lax
from jax.sharding import PartitionSpec as P


def on_device(tokens, codebook, codes):
    tok_rows = tokens.shape[0]
    width = tokens.shape[1]
    per_dev = codebook.shape[0]
    devices = lax.axis_size("row") * lax.axis_size("col")
    total_codes = per_dev * devices
    total_tokens = tok_rows * devices
    full_book = lax.all_gather(codebook, ("row", "col"), axis=0, tiled=True)
    quantized = jnp.take(full_book, codes, axis=0)
    diff = tokens.astype(jnp.float32) - quantized.astype(jnp.float32)
    token_loss = jnp.sum(diff * diff, axis=1) / width
    loss_part = jnp.sum(token_loss)
    local_counts = jax.ops.segment_sum(
        jnp.ones((tok_rows,), jnp.float32), codes, num_segments=total_codes
    )
    local_loss = jax.ops.segment_sum(token_loss, codes, num_segments=total_codes)
    floor_prob = jnp.float32(1.0 / total_tokens)
    totals, loss_totals = lax.psum((local_counts, local_loss), ("row", "col"))
    loss_sum = lax.psum(loss_part, ("row", "col"))
    probs = totals / total_tokens
    terms = jnp.where(
        totals > 0.5, probs * jnp.log(jnp.maximum(probs, floor_prob)), jnp.float32(0.0)
    )
    entropy = jnp.sum(terms)
    offset = lax.axis_index(("row", "col")) * per_dev
    owned_counts = lax.dynamic_slice_in_dim(totals, offset, per_dev, 0)
    code_loss = lax.dynamic_slice_in_dim(loss_totals, offset, per_dev, 0)
    code_counts = owned_counts.astype(jnp.int32)
    commitment = 0.25 * loss_sum / total_tokens
    perplexity = jnp.exp(-entropy)
    return (quantized, token_loss, code_counts, code_loss, commitment, perplexity)


def solution(mesh):
    return jax.shard_map(
        on_device,
        mesh=mesh,
        in_specs=(P(("row", "col"), None), P(("row", "col"), None), P(("row", "col"))),
        out_specs=(
            P(("row", "col"), None),
            P(("row", "col")),
            P(("row", "col")),
            P(("row", "col")),
            P(),
            P(),
        ),
        check_vma=False,
    )
```

profile of v0, /device:TPU:0, one launch (start us, length us, event | category | flops | bytes accessed | tf_op | source)
XLA Modules:
  0.0 242.8 jit_solution(13343456410854663029)
XLA Ops:
  7.2 0.0 all-gather.2.cloned.1.call-start
  7.2 0.7 all-gather.2.cloned.1.call-update
  7.9 0.0 all-reduce.3.cloned.1.call-start
  8.0 5.3 %scatter_custom_fusion = f32[16384]{0:T(1024)} fusion(s32[768]{0:T(1024)} %param.5, f32[768]{0:T(1024)S(1)} %broadcast.9, f32[]{:T(128)} %constant.18.clone.1), kind=kCustom, calls=%fused_computation.8 | custom fusion | flops 768 | bytes 66048 | tf_op jit(solution)/shard_map/scatter-add | solution.py:19
  13.3 0.7 compare_select_fusion
  14.0 0.7 compare_and_fusion
  14.7 76.0 %all-gather.2.cloned.1.call-done = bf16[16384,256]{1,0:T(8,128)(2,1)} async-done(((bf16[512,256]{1,0:T(8,128)(2,1)}), bf16[16384,256]{1,0:T(8,128)(2,1)}) %all-gather.2.cloned.1.call-update) | async-done | bytes 8388624 | tf_op jit(solution)/shard_map/all_gather | solution.py:14
  90.6 6.6 %gather_fusion = bf16[768,256]{1,0:T(8,128)(2,1)S(1)} fusion(bf16[16384,256]{1,0:T(8,128)(2,1)} %all-gather.2.cloned.1.call-done, s32[1024]{0:T(1024)S(1)} %pad_clamp_fusion), kind=kCustom, calls=%fused_computation | custom fusion | bytes 789504 | tf_op jit(solution)/shard_map/jit(_take)/gather | solution.py:15
  97.2 2.0 multiply_reduce_fusion
  99.2 0.6 fusion.4
  99.8 0.0 copy-start
  99.8 5.3 %scatter_custom_fusion.1 = f32[16384]{0:T(1024)} fusion(s32[768]{0:T(1024)} %param.5, f32[768]{0:T(1024)S(1)} %get-tuple-element.9, f32[]{:T(128)} %constant.18.clone.1), kind=kCustom, calls=%fused_computation.6 | custom fusion | flops 768 | bytes 66048 | tf_op jit(solution)/shard_map/scatter-add | solution.py:22
  105.1 0.0 all-reduce.3.cloned.1.call-update
  105.1 39.6 %psum.23 = f32[]{:T(128)} all-reduce(f32[]{:T(128)} %get-tuple-element.8), channel_id=1, replica_groups=mesh['row'=4,'col'=8] {'row','col'}, use_global_device_ids=true, to_apply=%region_6.7 | all-reduce | flops 1 | bytes 8 | tf_op jit(solution)/shard_map/psum | solution.py:25
  145.3 83.5 %all-reduce.3.cloned.1.call-done = (f32[16384]{0:T(1024)}, f32[16384]{0:T(1024)}) async-done(((f32[16384]{0:T(1024)}, f32[16384]{0:T(1024)}), (f32[16384]{0:T(1024)}, f32[16384]{0:T(1024)})) %all-reduce.3.cloned.1.call-update) | async-done | bytes 131088 | tf_op jit(solution)/shard_map/psum | solution.py:24
  228.9 1.5 select_reduce_fusion
  230.3 1.3 dynamic-slice_convert_fusion
  231.7 1.3 dynamic_slice.7
  233.7 0.0 copy-done
  (2 shorter events, 0.0 us)
Async XLA Ops:
  7.2 83.5 %all-gather.2.cloned.1.call-start = ((), (), s32[]{:S(2)}) async-start(), calls=%async_computation | async-start | bytes 8650752 | tf_op jit(solution)/shard_map/all_gather | solution.py:14
  7.9 221.0 %all-reduce.3.cloned.1.call-start = ((), (), s32[]{:S(2)}) async-start(), calls=%async_computation.1 | async-start | bytes 262144 | tf_op jit(solution)/shard_map/psum | solution.py:24
  99.8 133.9 %copy-start = (f32[768]{0:T(1024)}, f32[768]{0:T(1024)S(1)}, u32[]{:S(2)}) copy-start(f32[768]{0:T(1024)S(1)} %get-tuple-element.9) | copy-start | bytes 9220
Sparse Core Ops, SparseCore 0:
  10.8 79.7 all-gather.1
  105.2 123.5 all-reduce.2
where the time goes:
time: 243 us
  waiting for transfers between devices  160 us (66%)
  blocking collectives  39.6 us (16%)
  between operations  17.7 us (7%)
  other arithmetic  17.4 us (7%)
  local copies, waits for them, and re-layouts  7.89 us (3%)
    psum x1, waiting for transfers between devices, on_device(): totals, loss_totals = lax.psum((local_counts, local_loss), ('row', 'col'))  83.5 us
    all_gather x1, waiting for transfers between devices, on_device(): full_book = lax.all_gather(codebook, ('row', 'col'), axis=0, tiled=True)  76 us
    psum x1, blocking collectives, on_device(): loss_sum = lax.psum(loss_part, ('row', 'col'))  39.6 us
    gather x1, local copies, waits for them, and re-layouts, on_device(): quantized = jnp.take(full_book, codes, axis=0)  6.56 us
    scatter-add x1, other arithmetic, on_device(): jax.ops.segment_sum(jnp.ones((tok_rows,), jnp.float32), codes, num_segmen...  5.32 us
    scatter-add x1, other arithmetic, on_device(): jax.ops.segment_sum(token_loss, codes, num_segments=total_codes)  5.3 us
  transfers between devices with their start and end apart: 2, of which 2 were waited for; matrix products, arithmetic and copies ran while one was open for 3% of the time, Pallas kernels for 0%

commit v1 on v0

v1 whole, which is shorter than its diff:
```python
import functools

import jax
import jax.numpy as jnp
from jax import lax
from jax.experimental import pallas as pl
from jax.experimental.pallas import tpu as pltpu
from jax.sharding import PartitionSpec as P

AXES = ("row", "col")
LANES = 128
SLOTS = 32
F32 = jnp.float32
BF16 = jnp.bfloat16
VMEM = pl.BlockSpec(memory_space=pltpu.VMEM)
SMEM = pl.BlockSpec(memory_space=pltpu.SMEM)


def iota(shape, dim):
    return lax.broadcasted_iota(jnp.int32, shape, dim)


def ones_where(mask):
    return jnp.where(mask, F32(1.0), F32(0.0)).astype(BF16)


def dot(a, b, dims=((1,), (0,))):
    return lax.dot_general(a, b, (dims, ((), ())), preferred_element_type=F32)


def rank_within(present):
    width = present.shape[1]
    before = ones_where(iota((width, width), 0) < iota((width, width), 1))
    return dot(ones_where(present), before)


def rows_equal(ids, count):
    steps = iota((count, LANES), 0)
    return jnp.concatenate(
        [steps == ids[k : k + 1, :] for k in range(ids.shape[0])], axis=1
    )


def request_kernel(codes_ref, pay_ref, slot_ref, *, devices, per_dev, slots):
    codes = codes_ref[...]
    shift = per_dev.bit_length() - 1
    owner_mask = rows_equal(codes >> shift, devices)
    local = ones_where(rows_equal(codes & (per_dev - 1), per_dev))
    hist = dot(ones_where(owner_mask), local, ((1,), (1,)))
    present = hist > 0.5
    rank = rank_within(present)
    unique = jnp.sum(jnp.where(present, F32(1.0), F32(0.0)), axis=1, keepdims=True)
    most = jnp.max(unique, axis=0, keepdims=True)
    pay_ref[:, :LANES] = jnp.broadcast_to(most, (devices, LANES))
    pay_ref[:, LANES:] = hist
    capped = jnp.minimum(rank, F32(slots - 1)).astype(BF16)
    per_token = dot(capped, local)
    base = (iota(owner_mask.shape, 0) * slots).astype(F32)
    slot = jnp.sum(
        jnp.where(owner_mask, per_token + base, F32(0.0)), axis=0, keepdims=True
    )
    slot_ref[...] = jnp.zeros(slot_ref.shape, F32)
    for k in range(codes.shape[0]):
        slot_ref[k : k + 1, :] = slot[:, k * LANES : (k + 1) * LANES]


def serve_kernel(pay_ref, book_ref, send_ref, rank_ref, counts_ref, ent_ref, most_ref, *, slots, total_tokens):
    devices = pay_ref.shape[0]
    per_dev = book_ref.shape[0]
    hist = pay_ref[:, LANES:]
    most_ref[0, 0] = jnp.max(pay_ref[:, :LANES])
    present = hist > 0.5
    rank_ref[...] = jnp.where(present, rank_within(present), F32(-1.0))
    counts = jnp.sum(hist, axis=0, keepdims=True)
    counts_ref[...] = counts.astype(jnp.int32)
    probs = counts / total_tokens
    terms = jnp.where(
        counts > 0.5,
        probs * jnp.log(jnp.maximum(probs, F32(1.0 / total_tokens))),
        F32(0.0),
    )
    ent_ref[...] = jnp.broadcast_to(jnp.sum(terms, axis=1, keepdims=True), ent_ref.shape)
    book = book_ref[...]
    steps = iota((slots, per_dev), 0).astype(F32)

    def group(g, carry):
        ranks = rank_ref[pl.ds(pl.multiple_of(g * 8, 8), 8), :]
        pick = jnp.concatenate(
            [ones_where(steps == ranks[j : j + 1, :]) for j in range(8)], axis=0
        )
        rows = dot(pick, book).astype(BF16)
        send_ref[pl.ds(pl.multiple_of(g * 8 * slots, 8 * slots), 8 * slots), :] = rows
        return carry

    lax.fori_loop(0, devices // 8, group, 0)


def loss_kernel(slot_ref, tokens_ref, recv_ref, ent_ref, quant_ref, loss_ref, back_ref, *, slots, block):
    tok_rows, width = tokens_ref.shape
    chunks = tok_rows // LANES
    devices = back_ref.shape[0]
    slot = slot_ref[...]
    cols = slot.T
    steps = iota((LANES, block), 1).astype(F32)

    def gather(b, acc):
        first = (b * block).astype(F32) if recv_ref.shape[0] > block else F32(0.0)
        pick = jnp.concatenate(
            [ones_where(steps == cols[:, k : k + 1] - first) for k in range(chunks)],
            axis=0,
        )
        start = pl.multiple_of(b * block, block)
        return acc + dot(pick, recv_ref[pl.ds(start, block), :])

    steps_n = recv_ref.shape[0] // block
    if steps_n == 1:
        pick = jnp.concatenate(
            [ones_where(steps == cols[:, k : k + 1]) for k in range(chunks)], axis=0
        )
        quant = dot(pick, recv_ref[...])
    else:
        quant = lax.fori_loop(0, steps_n, gather, jnp.zeros((tok_rows, width), F32))
    quant_ref[...] = quant.astype(BF16)
    diff = tokens_ref[...].astype(F32) - quant
    loss = jnp.sum(diff * diff, axis=1, keepdims=True) / width
    total = jnp.sum(loss, axis=0, keepdims=True)
    rows = []
    for k in range(chunks):
        part = jnp.broadcast_to(loss[k * LANES : (k + 1) * LANES, :], (LANES, LANES))
        row = part.T[0:1, :]
        loss_ref[k : k + 1, :] = row
        rows.append(row)
    loss_row = jnp.concatenate(rows, axis=1)
    slot_int = slot.astype(jnp.int32)[:chunks]
    shift = slots.bit_length() - 1
    owner_mask = rows_equal(slot_int >> shift, devices)
    rank = ones_where(rows_equal(slot_int & (slots - 1), LANES))
    high = loss_row.astype(BF16).astype(F32)
    mid = (loss_row - high).astype(BF16).astype(F32)
    low = loss_row - high - mid
    sums = jnp.zeros((devices, LANES), F32)
    for piece in (low, mid, high):
        weighted = jnp.where(owner_mask, piece, F32(0.0)).astype(BF16)
        sums = sums + dot(weighted, rank, ((1,), (1,)))
    lane = iota((devices, LANES), 1)
    ent = jnp.broadcast_to(ent_ref[...], (devices, LANES))
    back_ref[...] = jnp.where(
        lane == slots, total, jnp.where(lane == slots + 1, ent, sums)
    )


def collect_kernel(back_ref, rank_ref, code_loss_ref, commit_ref, perp_ref, *, slots, total_tokens):
    devices, per_dev = rank_ref.shape

    def group(g, acc):
        at = pl.ds(pl.multiple_of(g * 8, 8), 8)
        ranks = rank_ref[at, :]
        back = back_ref[at, :]
        for r in range(slots):
            acc = acc + jnp.where(ranks == F32(r), back[:, r : r + 1], F32(0.0))
        return acc

    acc = lax.fori_loop(0, devices // 8, group, jnp.zeros((8, per_dev), F32))
    code_loss_ref[...] = jnp.sum(acc, axis=0, keepdims=True)
    sums = jnp.sum(back_ref[...], axis=0, keepdims=True)
    commit_ref[...] = 0.25 * sums[:, slots : slots + 1] / total_tokens
    perp_ref[...] = jnp.exp(-sums[:, slots + 1 : slots + 2])


def on_device(tokens, codebook, codes, *, devices):
    tok_rows, width = tokens.shape
    per_dev = codebook.shape[0]
    total_tokens = tok_rows * devices
    slots = min(SLOTS, per_dev)
    chunks = tok_rows // LANES
    n_slots = devices * slots
    shape = jax.ShapeDtypeStruct

    pay, slot = pl.pallas_call(
        functools.partial(request_kernel, devices=devices, per_dev=per_dev, slots=slots),
        out_shape=(
            shape((devices, LANES + per_dev), F32),
            shape((-(-chunks // 8) * 8, LANES), F32),
        ),
        in_specs=[VMEM],
        out_specs=(VMEM, VMEM),
        name="request",
    )(codes.reshape(chunks, LANES))
    pay_in = lax.all_to_all(pay, AXES, 0, 0, tiled=True)
    send, rank, counts, ent, most = pl.pallas_call(
        functools.partial(serve_kernel, slots=slots, total_tokens=total_tokens),
        out_shape=(
            shape((n_slots, width), BF16),
            shape((devices, per_dev), F32),
            shape((1, per_dev), jnp.int32),
            shape((1, LANES), F32),
            shape((1, 1), F32),
        ),
        in_specs=[VMEM, VMEM],
        out_specs=(VMEM, VMEM, VMEM, VMEM, SMEM),
        name="serve",
    )(pay_in, codebook)
    code_counts = counts.reshape(per_dev)

    def exchange_slots(tokens, codebook, codes, slot, send, rank, ent):
        recv = lax.all_to_all(send, AXES, 0, 0, tiled=True)
        quantized, loss, back = pl.pallas_call(
            functools.partial(loss_kernel, slots=slots, block=min(n_slots, 1024)),
            out_shape=(
                shape((tok_rows, width), BF16),
                shape((chunks, LANES), F32),
                shape((devices, LANES), F32),
            ),
            in_specs=[VMEM] * 4,
            out_specs=(VMEM,) * 3,
            name="losses",
        )(slot, tokens, recv, ent)
        back_in = lax.all_to_all(back, AXES, 0, 0, tiled=True)
        code_loss, commit, perp = pl.pallas_call(
            functools.partial(collect_kernel, slots=slots, total_tokens=total_tokens),
            out_shape=(shape((1, per_dev), F32), shape((1, 1), F32), shape((1, 1), F32)),
            in_specs=[VMEM] * 2,
            out_specs=(VMEM,) * 3,
            name="collect",
        )(back_in, rank)
        return (
            quantized,
            loss.reshape(tok_rows),
            code_loss.reshape(per_dev),
            commit.reshape(()),
            perp.reshape(()),
        )

    def exchange_book(tokens, codebook, codes, slot, send, rank, ent):
        spread = jnp.broadcast_to(codebook[None], (devices, per_dev, width))
        book = lax.all_to_all(spread, AXES, 0, 0, tiled=True)
        book = book.reshape(devices * per_dev, width)
        quantized = jnp.take(book, codes, axis=0, mode="clip")
        diff = tokens.astype(F32) - quantized.astype(F32)
        token_loss = jnp.sum(diff * diff, axis=1) / width
        part = jax.ops.segment_sum(token_loss, codes, num_segments=devices * per_dev)
        part = lax.all_to_all(part.reshape(devices, per_dev), AXES, 0, 0, tiled=True)
        lane = iota((devices, LANES), 1)
        pair = jnp.where(lane == 0, jnp.sum(token_loss), ent)
        sums = jnp.sum(lax.all_to_all(pair, AXES, 0, 0, tiled=True), axis=0)
        return (
            quantized,
            token_loss,
            jnp.sum(part, axis=0),
            0.25 * sums[0] / total_tokens,
            jnp.exp(-sums[1]),
        )

    quantized, token_loss, code_loss, commitment, perplexity = lax.cond(
        most[0, 0] > slots,
        exchange_book,
        exchange_slots,
        tokens, codebook, codes, slot, send, rank, ent,
    )
    return (quantized, token_loss, code_counts, code_loss, commitment, perplexity)


def solution(mesh):
    devices = mesh.shape["row"] * mesh.shape["col"]
    split = P(AXES)
    return jax.shard_map(
        functools.partial(on_device, devices=devices),
        mesh=mesh,
        in_specs=(P(AXES, None), P(AXES, None), split),
        out_specs=(P(AXES, None), split, split, split, P(), P()),
        check_vma=False,
    )
```

time: 243 us -> 55.9 us (0.23)
  waiting for transfers between devices: 160 us -> 0 us
  other arithmetic: 17.4 us -> 0 us
  between operations: 17.7 us -> 1.29 us
  Pallas kernels: 0 us -> 9.15 us
  local copies, waits for them, and re-layouts: 7.89 us -> 2.19 us
  blocking collectives: 39.6 us -> 42.9 us
    psum x1 -> x0, waiting for transfers between devices: 83.5 us -> none  [on_device(): totals, loss_totals = lax.psum((local_counts, local_loss), ('row', 'col'))]
    all_gather x1 -> x0, waiting for transfers between devices: 76 us -> none  [on_device(): full_book = lax.all_gather(codebook, ('row', 'col'), axis=0, tiled=True)]
    all_to_all x0 -> x3, blocking collectives: none -> 42.9 us  [the longest x1 18 us: exchange_slots(): recv = lax.all_to_all(send, AXES, 0, 0, tiled=True)]
    psum x1 -> x0, blocking collectives: 39.6 us -> none  [on_device(): loss_sum = lax.psum(loss_part, ('row', 'col'))]
    scatter-add x2 -> x0, other arithmetic: 10.6 us -> none  [the longest x1 5.32 us: on_device(): jax.ops.segment_sum(jnp.ones((tok_rows,), jnp.float32), codes, num_segmen...]
    pallas_call x0 -> x4, Pallas kernels: none -> 9.15 us  [the longest x1 3.1 us: exchange_slots(): pl.pallas_call(functools.partial(loss_kernel, slots=slots, block=min(n_sl...]
    gather x1 -> x0, local copies, waits for them, and re-layouts: 6.56 us -> none  [on_device(): quantized = jnp.take(full_book, codes, axis=0)]
    reduce_sum x3 -> x0, other arithmetic: 4.07 us -> none  [the longest x1 2 us: on_device(): token_loss = jnp.sum(diff * diff, axis=1) / width]
  transfers between devices with their start and end apart: 2 -> 0, of which waited for: 2 -> 0; matrix products, arithmetic and copies ran while one was open for 3% -> 0% of each run, Pallas kernels for 0% -> 0%
where the time goes in v1:
time: 55.9 us; the launch traced here: 55.5 us
  blocking collectives  42.9 us (77%)
  Pallas kernels  9.15 us (16%)
  local copies, waits for them, and re-layouts  2.19 us (4%)
  between operations  1.29 us (2%)
    all_to_all x1, blocking collectives, exchange_slots(): recv = lax.all_to_all(send, AXES, 0, 0, tiled=True)  18 us
    all_to_all x1, blocking collectives, on_device(): pay_in = lax.all_to_all(pay, AXES, 0, 0, tiled=True)  14.7 us
    all_to_all x1, blocking collectives, exchange_slots(): back_in = lax.all_to_all(back, AXES, 0, 0, tiled=True)  10.2 us
    pallas_call x1, Pallas kernels, exchange_slots(): pl.pallas_call(functools.partial(loss_kernel, slots=slots, block=min(n_sl...  3.1 us
    pallas_call x1, Pallas kernels, on_device(): pl.pallas_call(functools.partial(serve_kernel, slots=slots, total_tokens=...  2.48 us
    pallas_call x1, Pallas kernels, exchange_slots(): pl.pallas_call(functools.partial(collect_kernel, slots=slots, total_token...  1.8 us
    pallas_call x1, Pallas kernels, on_device(): pl.pallas_call(functools.partial(request_kernel, devices=devices, per_dev...  1.77 us
    unnamed x3, local copies, waits for them, and re-layouts  1.22 us

profile of v1, /device:TPU:0, one launch (start us, length us, event | category | flops | bytes accessed | tf_op | source)
XLA Modules:
  0.0 55.5 jit_solution(11463238057993714261)
XLA Ops:
  0.6 1.8 %request.1 = (f32[32,640]{1,0:T(8,128)}, f32[8,128]{1,0:T(8,128)S(1)}) custom-call(s32[6,128]{1,0:T(8,128)} %bitcast.30), custom_call_target="tpu_custom_call" | custom-call | tf_op jit(solution)/shard_map/request/pallas_call | solution.py:179
  2.4 1.0 %copy.16 = f32[32,1,640]{2,1,0:T(1,128)S(1)} copy(f32[32,1,640]{2,0,1:T(8,128)} %bitcast.26) | data formatting | bytes 163840 | tf_op jit(solution)/shard_map/all_to_all | solution.py:189
  3.4 14.7 %all_to_all.45 = f32[32,1,640]{2,1,0:T(1,128)S(1)} all-to-all(f32[32,1,640]{2,1,0:T(1,128)S(1)} %copy.16), channel_id=1, replica_groups=mesh['row'=4,'col'=8] {'row','col'}, dimensions={0} | all-to-all | bytes 163840 | tf_op jit(solution)/shard_map/all_to_all | solution.py:189
  18.1 0.6 %copy.20 = f32[32,1,640]{2,0,1:T(8,128)} copy(f32[32,1,640]{2,1,0:T(1,128)S(1)} %all_to_all.45) | data formatting | bytes 163840
  18.7 2.5 %serve.1 = (bf16[1024,256]{1,0:T(8,128)(2,1)S(1)}, f32[32,512]{1,0:T(8,128)S(1)}, s32[1,512]{1,0:T(1,128)}, f32[1,128]{1,0:T(1,128)S(1)}, f32[1,1]{1,0:T(1,128)}) custom-call(f32[32,640]{1,0:T(8,128)} %bitcast.25, bf16[512,256]{1,0:T(8,128)(2,1)} %book_ref.1), custom_call_target="tpu_custom_call" | custom-call | tf_op jit(solution)/shard_map/serve/pallas_call | solution.py:190
  21.9 33.1 %conditional.1 = (bf16[768,256]{1,0:T(8,128)(2,1)}, f32[768]{0:T(1024)}, f32[512]{0:T(512)S(1)}, f32[]{:T(128)}, f32[]{:T(128)}) conditional(s32[]{:T(128)} %bitcast.18, (bf16[1024,256]{1,0:T(8,128)(2,1)S(1)}, f32[8,128]{1,0:T(8,128)S(1)}, bf16[768,256]{1,0:T(8,128)(2,1)}, f32[1,128]{1,0:T(1,128)S(1)}, f32[32,512]{1,0:T(8,128)S(1)}) %tuple.16, ...), branch_computations={%region_0.0_spmd, %region_1.7_spmd} | conditional | flops 1009665 | bytes 37407740 | solution.py:254
  21.9 18.0 %all_to_all.43 = bf16[32,32,256]{2,1,0:T(8,128)(2,1)} all-to-all(bf16[32,32,256]{2,1,0:T(8,128)(2,1)S(1)} %bitcast.24), channel_id=1, replica_groups=mesh['row'=4,'col'=8] {'row','col'}, dimensions={0} | all-to-all | bytes 1048576 | tf_op jit(solution)/shard_map/cond/branch_0_fun/all_to_all | solution.py:206
  39.9 3.1 %losses.1 = (bf16[768,256]{1,0:T(8,128)(2,1)}, f32[6,128]{1,0:T(8,128)}, f32[32,128]{1,0:T(8,128)}) custom-call(f32[8,128]{1,0:T(8,128)S(1)} %get-tuple-element.18.slot_ref, bf16[768,256]{1,0:T(8,128)(2,1)} %get-tuple-element.19.tokens_ref, bf16[1024,256]{1,0:T(8,128)(2,1)} %bitcast.23, f32[1,128]{1,0:T(1,128)S(1)} %get-tuple-element.21.ent_ref), custom_call_target="tpu_custom_call" | custom-call | tf_op jit(solution)/shard_map/cond/branch_0_fun/losses/pallas_call | solution.py:207
  43.0 10.2 %all_to_all.44 = f32[32,1,128]{2,1,0:T(1,128)} all-to-all(f32[32,1,128]{2,1,0:T(1,128)} %bitcast.29), channel_id=1, replica_groups=mesh['row'=4,'col'=8] {'row','col'}, dimensions={0} | all-to-all | bytes 32768 | tf_op jit(solution)/shard_map/cond/branch_0_fun/all_to_all | solution.py:218
  53.1 1.8 %collect.1 = (f32[1,512]{1,0:T(1,128)S(1)}, f32[1,1]{1,0:T(1,128)}, f32[1,1]{1,0:T(1,128)}) custom-call(f32[32,128]{1,0:T(8,128)} %bitcast.27, f32[32,512]{1,0:T(8,128)S(1)} %get-tuple-element.25.rank_ref), custom_call_target="tpu_custom_call" | custom-call | tf_op jit(solution)/shard_map/cond/branch_0_fun/collect/pallas_call | solution.py:219
  54.9 0.0 copy-start.2
  54.9 0.6 %copy-done.2 = f32[512]{0:T(512)} copy-done((f32[512]{0:T(512)}, f32[512]{0:T(512)S(1)}, u32[]{:S(2)}) %copy-start.2) | copy-done | bytes 2072
Async XLA Ops:
  54.9 0.6 %copy-start.2 = (f32[512]{0:T(512)}, f32[512]{0:T(512)S(1)}, u32[]{:S(2)}) copy-start(f32[512]{0:T(512)S(1)} %get-tuple-element.48) | copy-start | bytes 6148

commit v2 on v1

--- a/solution.py
+++ b/solution.py
@@ -13,6 +13,7 @@
 F32 = jnp.float32
 BF16 = jnp.bfloat16
 VMEM = pl.BlockSpec(memory_space=pltpu.VMEM)
+ANY = pl.BlockSpec(memory_space=pl.ANY)
 SMEM = pl.BlockSpec(memory_space=pltpu.SMEM)
 
 
@@ -41,18 +42,22 @@
     )
 
 
-def request_kernel(codes_ref, pay_ref, slot_ref, *, devices, per_dev, slots):
+def request_kernel(codes_ref, tokens_ref, pay_ref, slot_ref, near_tokens_ref, sem, *, devices, per_dev, slots):
+    fetch_tokens = pltpu.make_async_copy(tokens_ref, near_tokens_ref, sem)
+    fetch_tokens.start()
     codes = codes_ref[...]
     shift = per_dev.bit_length() - 1
+    tiles = pay_ref.shape[0] // devices
     owner_mask = rows_equal(codes >> shift, devices)
-    local = ones_where(rows_equal(codes & (per_dev - 1), per_dev))
+    local = ones_where(rows_equal(codes & (per_dev - 1), tiles * LANES))
     hist = dot(ones_where(owner_mask), local, ((1,), (1,)))
     present = hist > 0.5
     rank = rank_within(present)
     unique = jnp.sum(jnp.where(present, F32(1.0), F32(0.0)), axis=1, keepdims=True)
     most = jnp.max(unique, axis=0, keepdims=True)
-    pay_ref[:, :LANES] = jnp.broadcast_to(most, (devices, LANES))
-    pay_ref[:, LANES:] = hist
+    coded = jnp.where(most > F32(slots), -1.0 - hist, hist)
+    for j in range(tiles):
+        pay_ref[pl.ds(j, devices, stride=tiles), :] = coded[:, j * LANES : (j + 1) * LANES]
     capped = jnp.minimum(rank, F32(slots - 1)).astype(BF16)
     per_token = dot(capped, local)
     base = (iota(owner_mask.shape, 0) * slots).astype(F32)
@@ -62,13 +67,20 @@
     slot_ref[...] = jnp.zeros(slot_ref.shape, F32)
     for k in range(codes.shape[0]):
         slot_ref[k : k + 1, :] = slot[:, k * LANES : (k + 1) * LANES]
-
-
-def serve_kernel(pay_ref, book_ref, send_ref, rank_ref, counts_ref, ent_ref, most_ref, *, slots, total_tokens):
-    devices = pay_ref.shape[0]
+    fetch_tokens.wait()
+
+
+def serve_kernel(pay_ref, book_ref, send_ref, rank_ref, counts_ref, ent_ref, least_ref, near_ref, sem, *, slots, total_tokens):
+    fetch = pltpu.make_async_copy(book_ref, near_ref, sem)
+    fetch.start()
+    devices = rank_ref.shape[0]
     per_dev = book_ref.shape[0]
-    hist = pay_ref[:, LANES:]
-    most_ref[0, 0] = jnp.max(pay_ref[:, :LANES])
+    tiles = pay_ref.shape[0] // devices
+    coded = jnp.concatenate(
+        [pay_ref[pl.ds(j, devices, stride=tiles), :] for j in range(tiles)], axis=1
+    )[:, :per_dev]
+    least_ref[0, 0] = jnp.min(coded)
+    hist = jnp.where(coded < 0.0, -1.0 - coded, coded)
     present = hist > 0.5
     rank_ref[...] = jnp.where(present, rank_within(present), F32(-1.0))
     counts = jnp.sum(hist, axis=0, keepdims=True)
@@ -80,7 +92,8 @@
         F32(0.0),
     )
     ent_ref[...] = jnp.broadcast_to(jnp.sum(terms, axis=1, keepdims=True), ent_ref.shape)
-    book = book_ref[...]
+    fetch.wait()
+    book = near_ref[...]
     steps = iota((slots, per_dev), 0).astype(F32)
 
     def group(g, carry):
@@ -95,42 +108,41 @@
     lax.fori_loop(0, devices // 8, group, 0)
 
 
-def loss_kernel(slot_ref, tokens_ref, recv_ref, ent_ref, quant_ref, loss_ref, back_ref, *, slots, block):
+def loss_kernel(slot_ref, tokens_ref, recv_ref, ent_ref, quant_ref, loss_ref, back_ref, near_ref, sems, *, slots, block):
     tok_rows, width = tokens_ref.shape
     chunks = tok_rows // LANES
     devices = back_ref.shape[0]
     slot = slot_ref[...]
     cols = slot.T
     steps = iota((LANES, block), 1).astype(F32)
-
-    def gather(b, acc):
-        first = (b * block).astype(F32) if recv_ref.shape[0] > block else F32(0.0)
-        pick = jnp.concatenate(
-            [ones_where(steps == cols[:, k : k + 1] - first) for k in range(chunks)],
-            axis=0,
-        )
-        start = pl.multiple_of(b * block, block)
-        return acc + dot(pick, recv_ref[pl.ds(start, block), :])
-
-    steps_n = recv_ref.shape[0] // block
-    if steps_n == 1:
-        pick = jnp.concatenate(
-            [ones_where(steps == cols[:, k : k + 1]) for k in range(chunks)], axis=0
-        )
-        quant = dot(pick, recv_ref[...])
-    else:
-        quant = lax.fori_loop(0, steps_n, gather, jnp.zeros((tok_rows, width), F32))
-    quant_ref[...] = quant.astype(BF16)
-    diff = tokens_ref[...].astype(F32) - quant
-    loss = jnp.sum(diff * diff, axis=1, keepdims=True) / width
-    total = jnp.sum(loss, axis=0, keepdims=True)
+    copies = []
     rows = []
     for k in range(chunks):
-        part = jnp.broadcast_to(loss[k * LANES : (k + 1) * LANES, :], (LANES, LANES))
-        row = part.T[0:1, :]
+        at = pl.ds(k * LANES, LANES)
+        col = cols[:, k : k + 1]
+        if recv_ref.shape[0] == block:
+            quant = dot(ones_where(steps == col), recv_ref[...])
+        else:
+
+            def gather(b, acc):
+                start = pl.multiple_of(b * block, block)
+                pick = ones_where(steps == col - (b * block).astype(F32))
+                return acc + dot(pick, recv_ref[pl.ds(start, block), :])
+
+            quant = lax.fori_loop(
+                0, recv_ref.shape[0] // block, gather, jnp.zeros((LANES, width), F32)
+            )
+        near_ref[at, :] = quant.astype(BF16)
+        copy = pltpu.make_async_copy(near_ref.at[at, :], quant_ref.at[at, :], sems.at[k])
+        copy.start()
+        copies.append(copy)
+        diff = tokens_ref[at, :].astype(F32) - quant
+        loss = jnp.sum(diff * diff, axis=1, keepdims=True) / width
+        row = jnp.broadcast_to(loss, (LANES, LANES)).T[0:1, :]
         loss_ref[k : k + 1, :] = row
         rows.append(row)
     loss_row = jnp.concatenate(rows, axis=1)
+    total = jnp.sum(loss_row, axis=1, keepdims=True)
     slot_int = slot.astype(jnp.int32)[:chunks]
     shift = slots.bit_length() - 1
     owner_mask = rows_equal(slot_int >> shift, devices)
@@ -138,15 +150,18 @@
     high = loss_row.astype(BF16).astype(F32)
     mid = (loss_row - high).astype(BF16).astype(F32)
     low = loss_row - high - mid
-    sums = jnp.zeros((devices, LANES), F32)
-    for piece in (low, mid, high):
-        weighted = jnp.where(owner_mask, piece, F32(0.0)).astype(BF16)
-        sums = sums + dot(weighted, rank, ((1,), (1,)))
+    weighted = jnp.concatenate(
+        [jnp.where(owner_mask, p, F32(0.0)).astype(BF16) for p in (low, mid, high)],
+        axis=1,
+    )
+    sums = dot(weighted, jnp.concatenate([rank] * 3, axis=1), ((1,), (1,)))
     lane = iota((devices, LANES), 1)
     ent = jnp.broadcast_to(ent_ref[...], (devices, LANES))
     back_ref[...] = jnp.where(
         lane == slots, total, jnp.where(lane == slots + 1, ent, sums)
     )
+    for copy in copies:
+        copy.wait()
 
 
 def collect_kernel(back_ref, rank_ref, code_loss_ref, commit_ref, perp_ref, *, slots, total_tokens):
@@ -156,12 +171,17 @@
         at = pl.ds(pl.multiple_of(g * 8, 8), 8)
         ranks = rank_ref[at, :]
         back = back_ref[at, :]
+        parts = [acc] + [jnp.zeros_like(acc)] * 3
         for r in range(slots):
-            acc = acc + jnp.where(ranks == F32(r), back[:, r : r + 1], F32(0.0))
-        return acc
+            term = jnp.where(ranks == F32(r), back[:, r : r + 1], F32(0.0))
+            parts[r % 4] = parts[r % 4] + term
+        return (parts[0] + parts[1]) + (parts[2] + parts[3])
 
     acc = lax.fori_loop(0, devices // 8, group, jnp.zeros((8, per_dev), F32))
-    code_loss_ref[...] = jnp.sum(acc, axis=0, keepdims=True)
+    code_loss = jnp.sum(acc, axis=0, keepdims=True)
+    lanes = code_loss_ref.shape[1]
+    for j in range(code_loss_ref.shape[0]):
+        code_loss_ref[j : j + 1, :] = code_loss[:, j * lanes : (j + 1) * lanes]
     sums = jnp.sum(back_ref[...], axis=0, keepdims=True)
     commit_ref[...] = 0.25 * sums[:, slots : slots + 1] / total_tokens
     perp_ref[...] = jnp.exp(-sums[:, slots + 1 : slots + 2])
@@ -176,18 +196,22 @@
     n_slots = devices * slots
     shape = jax.ShapeDtypeStruct
 
-    pay, slot = pl.pallas_call(
+    tiles = max(per_dev // LANES, 1)
+    pay, slot, near_tokens = pl.pallas_call(
         functools.partial(request_kernel, devices=devices, per_dev=per_dev, slots=slots),
         out_shape=(
-            shape((devices, LANES + per_dev), F32),
+            shape((devices * tiles, LANES), F32),
             shape((-(-chunks // 8) * 8, LANES), F32),
+            shape(tokens.shape, BF16),
         ),
-        in_specs=[VMEM],
-        out_specs=(VMEM, VMEM),
+        in_specs=[VMEM, ANY],
+        out_specs=(VMEM,) * 3,
+        scratch_shapes=[pltpu.SemaphoreType.DMA],
         name="request",
-    )(codes.reshape(chunks, LANES))
-    pay_in = lax.all_to_all(pay, AXES, 0, 0, tiled=True)
-    send, rank, counts, ent, most = pl.pallas_call(
+    )(codes.reshape(chunks, LANES), tokens)
+    pay_in = lax.all_to_all(pay.reshape(devices, tiles, LANES), AXES, 0, 0)
+    pay_in = pay_in.reshape(devices * tiles, LANES)
+    send, rank, counts, ent, least = pl.pallas_call(
         functools.partial(serve_kernel, slots=slots, total_tokens=total_tokens),
         out_shape=(
             shape((n_slots, width), BF16),
@@ -196,13 +220,14 @@
             shape((1, LANES), F32),
             shape((1, 1), F32),
         ),
-        in_specs=[VMEM, VMEM],
+        in_specs=[VMEM, ANY],
         out_specs=(VMEM, VMEM, VMEM, VMEM, SMEM),
+        scratch_shapes=[pltpu.VMEM(codebook.shape, BF16), pltpu.SemaphoreType.DMA],
         name="serve",
     )(pay_in, codebook)
     code_counts = counts.reshape(per_dev)
 
-    def exchange_slots(tokens, codebook, codes, slot, send, rank, ent):
+    def exchange_slots(tokens, near_tokens, codebook, codes, slot, send, rank, ent):
         recv = lax.all_to_all(send, AXES, 0, 0, tiled=True)
         quantized, loss, back = pl.pallas_call(
             functools.partial(loss_kernel, slots=slots, block=min(n_slots, 1024)),
@@ -212,13 +237,17 @@
                 shape((devices, LANES), F32),
             ),
             in_specs=[VMEM] * 4,
-            out_specs=(VMEM,) * 3,
+            out_specs=(ANY, VMEM, VMEM),
+            scratch_shapes=[
+                pltpu.VMEM((tok_rows, width), BF16),
+                pltpu.SemaphoreType.DMA((chunks,)),
+            ],
             name="losses",
-        )(slot, tokens, recv, ent)
+        )(slot, near_tokens, recv, ent)
         back_in = lax.all_to_all(back, AXES, 0, 0, tiled=True)
         code_loss, commit, perp = pl.pallas_call(
             functools.partial(collect_kernel, slots=slots, total_tokens=total_tokens),
-            out_shape=(shape((1, per_dev), F32), shape((1, 1), F32), shape((1, 1), F32)),
+            out_shape=(shape((tiles, per_dev // tiles), F32), shape((1, 1), F32), shape((1, 1), F32)),
             in_specs=[VMEM] * 2,
             out_specs=(VMEM,) * 3,
             name="collect",
@@ -231,7 +260,7 @@
             perp.reshape(()),
         )
 
-    def exchange_book(tokens, codebook, codes, slot, send, rank, ent):
+    def exchange_book(tokens, near_tokens, codebook, codes, slot, send, rank, ent):
         spread = jnp.broadcast_to(codebook[None], (devices, per_dev, width))
         book = lax.all_to_all(spread, AXES, 0, 0, tiled=True)
         book = book.reshape(devices * per_dev, width)
@@ -252,10 +281,10 @@
         )
 
     quantized, token_loss, code_loss, commitment, perplexity = lax.cond(
-        most[0, 0] > slots,
+        least[0, 0] < 0.0,
         exchange_book,
         exchange_slots,
-        tokens, codebook, codes, slot, send, rank, ent,
+        tokens, near_tokens, codebook, codes, slot, send, rank, ent,
     )
     return (quantized, token_loss, code_counts, code_loss, commitment, perplexity)
 

time: 55.9 us -> 55.8 us (level)
  local copies, waits for them, and re-layouts: 2.19 us -> 0.58 us
  Pallas kernels: 9.15 us -> 10.4 us
    all_to_all x1 -> x0, local copies, waits for them, and re-layouts: 0.97 us -> none  [on_device(): pay_in = lax.all_to_all(pay, AXES, 0, 0, tiled=True)]
    unnamed x3 -> x2, local copies, waits for them, and re-layouts: 1.22 us -> 0.58 us
    pallas_call x1, Pallas kernels: 2.48 us -> 3.12 us  [on_device(): pl.pallas_call(functools.partial(serve_kernel, slots=slots, total_tokens=...]
where the time goes in v2:
time: 55.8 us; the launch traced here: 55.3 us
  blocking collectives  43 us (77%)
  Pallas kernels  10.4 us (19%)
  between operations  1.3 us (2%)
  local copies, waits for them, and re-layouts  0.58 us (1%)
    all_to_all x1, blocking collectives, exchange_slots(): recv = lax.all_to_all(send, AXES, 0, 0, tiled=True)  18 us
    all_to_all x1, blocking collectives, on_device(): pay_in = lax.all_to_all(pay.reshape(devices, tiles, LANES), AXES, 0, 0)  14.9 us
    all_to_all x1, blocking collectives, exchange_slots(): back_in = lax.all_to_all(back, AXES, 0, 0, tiled=True)  10.2 us
    pallas_call x1, Pallas kernels, exchange_slots(): pl.pallas_call(functools.partial(loss_kernel, slots=slots, block=min(n_sl...  3.12 us
    pallas_call x1, Pallas kernels, on_device(): pl.pallas_call(functools.partial(serve_kernel, slots=slots, total_tokens=...  3.12 us
    pallas_call x1, Pallas kernels, on_device(): pl.pallas_call(functools.partial(request_kernel, devices=devices, per_dev...  2.32 us
    pallas_call x1, Pallas kernels, exchange_slots(): pl.pallas_call(functools.partial(collect_kernel, slots=slots, total_token...  1.84 us

profile of v2, /device:TPU:0, one launch (start us, length us, event | category | flops | bytes accessed | tf_op | source)
XLA Modules:
  0.0 55.3 jit_solution(2571120561175652116)
XLA Ops:
  0.6 2.3 %request.1 = (f32[128,128]{1,0:T(8,128)}, f32[8,128]{1,0:T(8,128)S(1)}, bf16[768,256]{1,0:T(8,128)(2,1)S(1)}) custom-call(s32[6,128]{1,0:T(8,128)} %bitcast.27, bf16[768,256]{1,0:T(8,128)(2,1)} %tokens_ref.1), custom_call_target="tpu_custom_call" | custom-call | tf_op jit(solution)/shard_map/request/pallas_call | solution.py:200
  3.0 14.9 %all_to_all.39 = f32[32,4,128]{2,1,0:T(4,128)} all-to-all(f32[32,4,128]{2,1,0:T(4,128)} %bitcast.25), channel_id=1, replica_groups=mesh['row'=4,'col'=8] {'row','col'}, dimensions={0} | all-to-all | bytes 131072 | tf_op jit(solution)/shard_map/all_to_all | solution.py:212
  17.8 3.1 %serve.1 = (bf16[1024,256]{1,0:T(8,128)(2,1)S(1)}, f32[32,512]{1,0:T(8,128)S(1)}, s32[1,512]{1,0:T(1,128)}, f32[1,128]{1,0:T(1,128)S(1)}, f32[1,1]{1,0:T(1,128)}) custom-call(f32[128,128]{1,0:T(8,128)} %bitcast.23, bf16[512,256]{1,0:T(8,128)(2,1)} %book_ref.1), custom_call_target="tpu_custom_call" | custom-call | tf_op jit(solution)/shard_map/serve/pallas_call | solution.py:214
  21.6 33.2 %conditional.1 = (bf16[768,256]{1,0:T(8,128)(2,1)}, f32[768]{0:T(1024)}, f32[512]{0:T(512)S(1)}, f32[]{:T(128)}, f32[]{:T(128)}) conditional(s32[]{:T(128)} %bitcast.19, (bf16[1024,256]{1,0:T(8,128)(2,1)S(1)}, f32[8,128]{1,0:T(8,128)S(1)}, bf16[768,256]{1,0:T(8,128)(2,1)S(1)}, f32[1,128]{1,0:T(1,128)S(1)}, f32[32,512]{1,0:T(8,128)S(1)}) %tuple.16, ...), branch_computations={%region_0.0_spmd, %region_1.7_spmd} | conditional | flops 1009665 | bytes 37407740 | solution.py:283
  21.6 18.0 %all_to_all.37 = bf16[32,32,256]{2,1,0:T(8,128)(2,1)} all-to-all(bf16[32,32,256]{2,1,0:T(8,128)(2,1)S(1)} %bitcast.22), channel_id=1, replica_groups=mesh['row'=4,'col'=8] {'row','col'}, dimensions={0} | all-to-all | bytes 1048576 | tf_op jit(solution)/shard_map/cond/branch_0_fun/all_to_all | solution.py:231
  39.6 3.1 %losses.1 = (bf16[768,256]{1,0:T(8,128)(2,1)}, f32[6,128]{1,0:T(8,128)}, f32[32,128]{1,0:T(8,128)}) custom-call(f32[8,128]{1,0:T(8,128)S(1)} %get-tuple-element.18.slot_ref, bf16[768,256]{1,0:T(8,128)(2,1)S(1)} %get-tuple-element.19.tokens_ref, bf16[1024,256]{1,0:T(8,128)(2,1)} %bitcast.21, f32[1,128]{1,0:T(1,128)S(1)} %get-tuple-element.21.ent_ref), custom_call_target="tpu_custom_call" | custom-call | tf_op jit(solution)/shard_map/cond/branch_0_fun/losses/pallas_call | solution.py:232
  42.7 10.2 %all_to_all.38 = f32[32,1,128]{2,1,0:T(1,128)} all-to-all(f32[32,1,128]{2,1,0:T(1,128)} %bitcast.28), channel_id=1, replica_groups=mesh['row'=4,'col'=8] {'row','col'}, dimensions={0} | all-to-all | bytes 32768 | tf_op jit(solution)/shard_map/cond/branch_0_fun/all_to_all | solution.py:247
  52.9 1.8 %collect.1 = (f32[4,128]{1,0:T(4,128)S(1)}, f32[1,1]{1,0:T(1,128)}, f32[1,1]{1,0:T(1,128)}) custom-call(f32[32,128]{1,0:T(8,128)} %bitcast.24, f32[32,512]{1,0:T(8,128)S(1)} %get-tuple-element.25.rank_ref), custom_call_target="tpu_custom_call" | custom-call | tf_op jit(solution)/shard_map/cond/branch_0_fun/collect/pallas_call | solution.py:248
  54.8 0.0 copy-start.2
  54.8 0.6 %copy-done.2 = f32[512]{0:T(512)} copy-done((f32[512]{0:T(512)}, f32[512]{0:T(512)S(1)}, u32[]{:S(2)}) %copy-start.2) | copy-done | bytes 2072
Async XLA Ops:
  54.8 0.6 %copy-start.2 = (f32[512]{0:T(512)}, f32[512]{0:T(512)S(1)}, u32[]{:S(2)}) copy-start(f32[512]{0:T(512)S(1)} %get-tuple-element.49) | copy-start | bytes 6148

commit v3 on v2

--- a/solution.py
+++ b/solution.py
@@ -29,10 +29,24 @@
     return lax.dot_general(a, b, (dims, ((), ())), preferred_element_type=F32)
 
 
-def rank_within(present):
-    width = present.shape[1]
-    before = ones_where(iota((width, width), 0) < iota((width, width), 1))
-    return dot(ones_where(present), before)
+def fold(x, rows):
+    while x.shape[0] > rows:
+        half = x.shape[0] // 2
+        x = x[:half] + x[half:]
+    return x
+
+
+def rank_within(present, tiles):
+    ones = ones_where(present)
+    lane = (LANES, LANES)
+    rank = dot(ones, ones_where(iota(lane, 0) < iota(lane, 1)))
+    unique = jnp.sum(jnp.where(present, F32(1.0), F32(0.0)), axis=1, keepdims=True)
+    row = iota(unique.shape, 0) & (tiles - 1)
+    earlier = jnp.zeros_like(unique)
+    for j in range(1, tiles):
+        moved = pltpu.roll(jnp.broadcast_to(unique, present.shape), j, 0)[:, :1]
+        earlier = earlier + jnp.where(row >= j, moved, F32(0.0))
+    return rank + earlier, unique + earlier
 
 
 def rows_equal(ids, count):
@@ -46,23 +60,21 @@
     fetch_tokens = pltpu.make_async_copy(tokens_ref, near_tokens_ref, sem)
     fetch_tokens.start()
     codes = codes_ref[...]
-    shift = per_dev.bit_length() - 1
     tiles = pay_ref.shape[0] // devices
-    owner_mask = rows_equal(codes >> shift, devices)
-    local = ones_where(rows_equal(codes & (per_dev - 1), tiles * LANES))
-    hist = dot(ones_where(owner_mask), local, ((1,), (1,)))
-    present = hist > 0.5
-    rank = rank_within(present)
-    unique = jnp.sum(jnp.where(present, F32(1.0), F32(0.0)), axis=1, keepdims=True)
+    span = per_dev // tiles
+    row_mask = rows_equal(codes >> (span.bit_length() - 1), devices * tiles)
+    lanes = ones_where(rows_equal(codes & (span - 1), LANES))
+    hist = dot(ones_where(row_mask), lanes, ((1,), (1,)))
+    rank, unique = rank_within(hist > 0.5, tiles)
     most = jnp.max(unique, axis=0, keepdims=True)
-    coded = jnp.where(most > F32(slots), -1.0 - hist, hist)
-    for j in range(tiles):
-        pay_ref[pl.ds(j, devices, stride=tiles), :] = coded[:, j * LANES : (j + 1) * LANES]
+    pay_ref[...] = jnp.where(most > F32(slots), -1.0 - hist, hist)
     capped = jnp.minimum(rank, F32(slots - 1)).astype(BF16)
-    per_token = dot(capped, local)
-    base = (iota(owner_mask.shape, 0) * slots).astype(F32)
+    per_token = dot(capped, lanes)
+    owner = iota(row_mask.shape, 0) >> (tiles.bit_length() - 1)
     slot = jnp.sum(
-        jnp.where(owner_mask, per_token + base, F32(0.0)), axis=0, keepdims=True
+        jnp.where(row_mask, per_token + (owner * slots).astype(F32), F32(0.0)),
+        axis=0,
+        keepdims=True,
     )
     slot_ref[...] = jnp.zeros(slot_ref.shape, F32)
     for k in range(codes.shape[0]):
@@ -73,39 +85,49 @@
 def serve_kernel(pay_ref, book_ref, send_ref, rank_ref, counts_ref, ent_ref, least_ref, near_ref, sem, *, slots, total_tokens):
     fetch = pltpu.make_async_copy(book_ref, near_ref, sem)
     fetch.start()
-    devices = rank_ref.shape[0]
     per_dev = book_ref.shape[0]
-    tiles = pay_ref.shape[0] // devices
-    coded = jnp.concatenate(
-        [pay_ref[pl.ds(j, devices, stride=tiles), :] for j in range(tiles)], axis=1
-    )[:, :per_dev]
+    tiles = counts_ref.shape[0]
+    span = per_dev // tiles
+    devices = pay_ref.shape[0] // tiles
+    coded = pay_ref[...]
     least_ref[0, 0] = jnp.min(coded)
     hist = jnp.where(coded < 0.0, -1.0 - coded, coded)
     present = hist > 0.5
-    rank_ref[...] = jnp.where(present, rank_within(present), F32(-1.0))
-    counts = jnp.sum(hist, axis=0, keepdims=True)
-    counts_ref[...] = counts.astype(jnp.int32)
+    rank_ref[...] = jnp.where(present, rank_within(present, tiles)[0], F32(-1.0))
+    fetch.wait()
+    book = near_ref[...]
+    steps = iota((slots, LANES), 0).astype(F32)
+
+    def group(g, carry):
+        ranks = rank_ref[pl.ds(pl.multiple_of(g * 8 * tiles, 8), 8 * tiles), :]
+        pick = jnp.concatenate(
+            [
+                jnp.concatenate(
+                    [
+                        ones_where(steps == ranks[i * tiles + j : i * tiles + j + 1, :])
+                        for j in range(tiles)
+                    ],
+                    axis=1,
+                )
+                for i in range(8)
+            ],
+            axis=0,
+        )
+        rows = dot(pick[:, :per_dev], book).astype(BF16)
+        send_ref[pl.ds(pl.multiple_of(g * 8 * slots, 8 * slots), 8 * slots), :] = rows
+        return carry
+
+    lax.fori_loop(0, devices // 8, group, 0, unroll=True if devices <= 32 else 1)
+    counts = fold(hist, tiles)
+    counts_ref[...] = counts[:, :span].astype(jnp.int32)
     probs = counts / total_tokens
     terms = jnp.where(
         counts > 0.5,
         probs * jnp.log(jnp.maximum(probs, F32(1.0 / total_tokens))),
         F32(0.0),
     )
-    ent_ref[...] = jnp.broadcast_to(jnp.sum(terms, axis=1, keepdims=True), ent_ref.shape)
-    fetch.wait()
-    book = near_ref[...]
-    steps = iota((slots, per_dev), 0).astype(F32)
-
-    def group(g, carry):
-        ranks = rank_ref[pl.ds(pl.multiple_of(g * 8, 8), 8), :]
-        pick = jnp.concatenate(
-            [ones_where(steps == ranks[j : j + 1, :]) for j in range(8)], axis=0
-        )
-        rows = dot(pick, book).astype(BF16)
-        send_ref[pl.ds(pl.multiple_of(g * 8 * slots, 8 * slots), 8 * slots), :] = rows
-        return carry
-
-    lax.fori_loop(0, devices // 8, group, 0)
+    ent = jnp.sum(jnp.sum(terms, axis=1, keepdims=True), axis=0, keepdims=True)
+    ent_ref[...] = jnp.broadcast_to(ent, ent_ref.shape)
 
 
 def loss_kernel(slot_ref, tokens_ref, recv_ref, ent_ref, quant_ref, loss_ref, back_ref, near_ref, sems, *, slots, block):
@@ -116,32 +138,43 @@
     cols = slot.T
     steps = iota((LANES, block), 1).astype(F32)
     copies = []
-    rows = []
-    for k in range(chunks):
-        at = pl.ds(k * LANES, LANES)
-        col = cols[:, k : k + 1]
+    lane = iota((LANES, LANES), 1)
+    losses = jnp.zeros((LANES, LANES), F32)
+    per_half = chunks // 2
+    for half in range(2):
+        at = pl.ds(half * per_half * LANES, per_half * LANES)
+        near = range(half * per_half, (half + 1) * per_half)
+
+        def pick(first):
+            return jnp.concatenate(
+                [ones_where(steps == cols[:, k : k + 1] - first) for k in near], axis=0
+            )
+
         if recv_ref.shape[0] == block:
-            quant = dot(ones_where(steps == col), recv_ref[...])
+            quant = dot(pick(F32(0.0)), recv_ref[...])
         else:
 
             def gather(b, acc):
                 start = pl.multiple_of(b * block, block)
-                pick = ones_where(steps == col - (b * block).astype(F32))
-                return acc + dot(pick, recv_ref[pl.ds(start, block), :])
+                return acc + dot(pick((b * block).astype(F32)), recv_ref[pl.ds(start, block), :])
 
             quant = lax.fori_loop(
-                0, recv_ref.shape[0] // block, gather, jnp.zeros((LANES, width), F32)
+                0,
+                recv_ref.shape[0] // block,
+                gather,
+                jnp.zeros((per_half * LANES, width), F32),
             )
         near_ref[at, :] = quant.astype(BF16)
-        copy = pltpu.make_async_copy(near_ref.at[at, :], quant_ref.at[at, :], sems.at[k])
+        copy = pltpu.make_async_copy(near_ref.at[at, :], quant_ref.at[at, :], sems.at[half])
         copy.start()
         copies.append(copy)
         diff = tokens_ref[at, :].astype(F32) - quant
         loss = jnp.sum(diff * diff, axis=1, keepdims=True) / width
-        row = jnp.broadcast_to(loss, (LANES, LANES)).T[0:1, :]
-        loss_ref[k : k + 1, :] = row
-        rows.append(row)
-    loss_row = jnp.concatenate(rows, axis=1)
+        for i, k in enumerate(near):
+            losses = jnp.where(lane == k, loss[i * LANES : (i + 1) * LANES, :], losses)
+    turned = losses.T
+    loss_ref[...] = turned[:chunks, :]
+    loss_row = jnp.concatenate([turned[k : k + 1, :] for k in range(chunks)], axis=1)
     total = jnp.sum(loss_row, axis=1, keepdims=True)
     slot_int = slot.astype(jnp.int32)[:chunks]
     shift = slots.bit_length() - 1
@@ -165,23 +198,21 @@
 
 
 def collect_kernel(back_ref, rank_ref, code_loss_ref, commit_ref, perp_ref, *, slots, total_tokens):
-    devices, per_dev = rank_ref.shape
-
-    def group(g, acc):
-        at = pl.ds(pl.multiple_of(g * 8, 8), 8)
-        ranks = rank_ref[at, :]
-        back = back_ref[at, :]
-        parts = [acc] + [jnp.zeros_like(acc)] * 3
-        for r in range(slots):
-            term = jnp.where(ranks == F32(r), back[:, r : r + 1], F32(0.0))
-            parts[r % 4] = parts[r % 4] + term
-        return (parts[0] + parts[1]) + (parts[2] + parts[3])
-
-    acc = lax.fori_loop(0, devices // 8, group, jnp.zeros((8, per_dev), F32))
-    code_loss = jnp.sum(acc, axis=0, keepdims=True)
-    lanes = code_loss_ref.shape[1]
-    for j in range(code_loss_ref.shape[0]):
-        code_loss_ref[j : j + 1, :] = code_loss[:, j * lanes : (j + 1) * lanes]
+    devices = back_ref.shape[0]
+    tiles = code_loss_ref.shape[0]
+    back = back_ref[...]
+    high = back.astype(BF16).astype(F32)
+    mid = (back - high).astype(BF16).astype(F32)
+    parts = jnp.concatenate(
+        [p.astype(BF16) for p in (back - high - mid, mid, high)], axis=0
+    )
+    shape = (devices * tiles, devices)
+    repeat = ones_where((iota(shape, 0) >> (tiles.bit_length() - 1)) == iota(shape, 1))
+    spread = dot(jnp.concatenate([repeat] * 3, axis=1), parts)
+    rank = rank_ref[...].astype(jnp.int32)
+    found = jnp.take_along_axis(spread, jnp.maximum(rank, 0), axis=1)
+    code_loss = fold(jnp.where(rank >= 0, found, F32(0.0)), tiles)
+    code_loss_ref[...] = code_loss[:, : code_loss_ref.shape[1]]
     sums = jnp.sum(back_ref[...], axis=0, keepdims=True)
     commit_ref[...] = 0.25 * sums[:, slots : slots + 1] / total_tokens
     perp_ref[...] = jnp.exp(-sums[:, slots + 1 : slots + 2])
@@ -215,8 +246,8 @@
         functools.partial(serve_kernel, slots=slots, total_tokens=total_tokens),
         out_shape=(
             shape((n_slots, width), BF16),
-            shape((devices, per_dev), F32),
-            shape((1, per_dev), jnp.int32),
+            shape((devices * tiles, LANES), F32),
+            shape((tiles, per_dev // tiles), jnp.int32),
             shape((1, LANES), F32),
             shape((1, 1), F32),
         ),
@@ -240,7 +271,7 @@
             out_specs=(ANY, VMEM, VMEM),
             scratch_shapes=[
                 pltpu.VMEM((tok_rows, width), BF16),
-                pltpu.SemaphoreType.DMA((chunks,)),
+                pltpu.SemaphoreType.DMA((2,)),
             ],
             name="losses",
         )(slot, near_tokens, recv, ent)

time: 55.8 us -> 55.1 us (0.987)
  Pallas kernels: 10.4 us -> 9.71 us
where the time goes in v3:
time: 55.1 us; the launch traced here: 54.6 us
  blocking collectives  43 us (78%)
  Pallas kernels  9.71 us (18%)
  between operations  1.3 us (2%)
  local copies, waits for them, and re-layouts  0.58 us (1%)
    all_to_all x1, blocking collectives, exchange_slots(): recv = lax.all_to_all(send, AXES, 0, 0, tiled=True)  18 us
    all_to_all x1, blocking collectives, on_device(): pay_in = lax.all_to_all(pay.reshape(devices, tiles, LANES), AXES, 0, 0)  14.9 us
    all_to_all x1, blocking collectives, exchange_slots(): back_in = lax.all_to_all(back, AXES, 0, 0, tiled=True)  10.2 us
    pallas_call x1, Pallas kernels, exchange_slots(): pl.pallas_call(functools.partial(loss_kernel, slots=slots, block=min(n_sl...  3.16 us
    pallas_call x1, Pallas kernels, on_device(): pl.pallas_call(functools.partial(serve_kernel, slots=slots, total_tokens=...  2.69 us
    pallas_call x1, Pallas kernels, on_device(): pl.pallas_call(functools.partial(request_kernel, devices=devices, per_dev...  2.32 us
    pallas_call x1, Pallas kernels, exchange_slots(): pl.pallas_call(functools.partial(collect_kernel, slots=slots, total_token...  1.53 us

profile of v3, /device:TPU:0, one launch (start us, length us, event | category | flops | bytes accessed | tf_op | source)
XLA Modules:
  0.0 54.6 jit_solution(14333925482799138013)
XLA Ops:
  0.6 2.3 %request.1 = (f32[128,128]{1,0:T(8,128)}, f32[8,128]{1,0:T(8,128)S(1)}, bf16[768,256]{1,0:T(8,128)(2,1)S(1)}) custom-call(s32[6,128]{1,0:T(8,128)} %bitcast.27, bf16[768,256]{1,0:T(8,128)(2,1)} %tokens_ref.1), custom_call_target="tpu_custom_call" | custom-call | tf_op jit(solution)/shard_map/request/pallas_call | solution.py:231
  3.0 14.9 %all_to_all.39 = f32[32,4,128]{2,1,0:T(4,128)} all-to-all(f32[32,4,128]{2,1,0:T(4,128)} %bitcast.25), channel_id=1, replica_groups=mesh['row'=4,'col'=8] {'row','col'}, dimensions={0} | all-to-all | bytes 131072 | tf_op jit(solution)/shard_map/all_to_all | solution.py:243
  17.8 2.7 %serve.1 = (bf16[1024,256]{1,0:T(8,128)(2,1)S(1)}, f32[128,128]{1,0:T(8,128)S(1)}, s32[4,128]{1,0:T(4,128)}, f32[1,128]{1,0:T(1,128)S(1)}, f32[1,1]{1,0:T(1,128)}) custom-call(f32[128,128]{1,0:T(8,128)} %bitcast.23, bf16[512,256]{1,0:T(8,128)(2,1)} %book_ref.1), custom_call_target="tpu_custom_call" | custom-call | tf_op jit(solution)/shard_map/serve/pallas_call | solution.py:245
  21.2 32.9 %conditional.1 = (bf16[768,256]{1,0:T(8,128)(2,1)}, f32[768]{0:T(1024)}, f32[512]{0:T(512)S(1)}, f32[]{:T(128)}, f32[]{:T(128)}) conditional(s32[]{:T(128)} %bitcast.19, (bf16[1024,256]{1,0:T(8,128)(2,1)S(1)}, f32[8,128]{1,0:T(8,128)S(1)}, bf16[768,256]{1,0:T(8,128)(2,1)S(1)}, f32[1,128]{1,0:T(1,128)S(1)}, f32[128,128]{1,0:T(8,128)S(1)}) %tuple.16, ...), branch_computations={%region_0.0_spmd, %region_1.7_spmd} | conditional | flops 1009665 | bytes 37407740 | solution.py:314
  21.2 18.0 %all_to_all.37 = bf16[32,32,256]{2,1,0:T(8,128)(2,1)} all-to-all(bf16[32,32,256]{2,1,0:T(8,128)(2,1)S(1)} %bitcast.22), channel_id=1, replica_groups=mesh['row'=4,'col'=8] {'row','col'}, dimensions={0} | all-to-all | bytes 1048576 | tf_op jit(solution)/shard_map/cond/branch_0_fun/all_to_all | solution.py:262
  39.2 3.2 %losses.1 = (bf16[768,256]{1,0:T(8,128)(2,1)}, f32[6,128]{1,0:T(8,128)}, f32[32,128]{1,0:T(8,128)}) custom-call(f32[8,128]{1,0:T(8,128)S(1)} %get-tuple-element.18.slot_ref, bf16[768,256]{1,0:T(8,128)(2,1)S(1)} %get-tuple-element.19.tokens_ref, bf16[1024,256]{1,0:T(8,128)(2,1)} %bitcast.21, f32[1,128]{1,0:T(1,128)S(1)} %get-tuple-element.21.ent_ref), custom_call_target="tpu_custom_call" | custom-call | tf_op jit(solution)/shard_map/cond/branch_0_fun/losses/pallas_call | solution.py:263
  42.4 10.2 %all_to_all.38 = f32[32,1,128]{2,1,0:T(1,128)} all-to-all(f32[32,1,128]{2,1,0:T(1,128)} %bitcast.28), channel_id=1, replica_groups=mesh['row'=4,'col'=8] {'row','col'}, dimensions={0} | all-to-all | bytes 32768 | tf_op jit(solution)/shard_map/cond/branch_0_fun/all_to_all | solution.py:278
  52.5 1.5 %collect.1 = (f32[4,128]{1,0:T(4,128)S(1)}, f32[1,1]{1,0:T(1,128)}, f32[1,1]{1,0:T(1,128)}) custom-call(f32[32,128]{1,0:T(8,128)} %bitcast.24, f32[128,128]{1,0:T(8,128)S(1)} %get-tuple-element.25.rank_ref), custom_call_target="tpu_custom_call" | custom-call | tf_op jit(solution)/shard_map/cond/branch_0_fun/collect/pallas_call | solution.py:279
  54.1 0.0 copy-start.2
  54.1 0.6 %copy-done.2 = f32[512]{0:T(512)} copy-done((f32[512]{0:T(512)}, f32[512]{0:T(512)S(1)}, u32[]{:S(2)}) %copy-start.2) | copy-done | bytes 2072
Async XLA Ops:
  54.1 0.6 %copy-start.2 = (f32[512]{0:T(512)}, f32[512]{0:T(512)S(1)}, u32[]{:S(2)}) copy-start(f32[512]{0:T(512)S(1)} %get-tuple-element.49) | copy-start | bytes 6148

commit v4 on v3

--- a/solution.py
+++ b/solution.py
@@ -56,9 +56,7 @@
     )
 
 
-def request_kernel(codes_ref, tokens_ref, pay_ref, slot_ref, near_tokens_ref, sem, *, devices, per_dev, slots):
-    fetch_tokens = pltpu.make_async_copy(tokens_ref, near_tokens_ref, sem)
-    fetch_tokens.start()
+def request_kernel(codes_ref, pay_ref, slot_ref, *, devices, per_dev, slots):
     codes = codes_ref[...]
     tiles = pay_ref.shape[0] // devices
     span = per_dev // tiles
@@ -79,7 +77,6 @@
     slot_ref[...] = jnp.zeros(slot_ref.shape, F32)
     for k in range(codes.shape[0]):
         slot_ref[k : k + 1, :] = slot[:, k * LANES : (k + 1) * LANES]
-    fetch_tokens.wait()
 
 
 def serve_kernel(pay_ref, book_ref, send_ref, rank_ref, counts_ref, ent_ref, least_ref, near_ref, sem, *, slots, total_tokens):
@@ -130,7 +127,9 @@
     ent_ref[...] = jnp.broadcast_to(ent, ent_ref.shape)
 
 
-def loss_kernel(slot_ref, tokens_ref, recv_ref, ent_ref, quant_ref, loss_ref, back_ref, near_ref, sems, *, slots, block):
+def loss_kernel(slot_ref, tokens_ref, recv_ref, ent_ref, quant_ref, loss_ref, back_ref, near_ref, near_tokens_ref, sems, *, slots, block):
+    fetch = pltpu.make_async_copy(tokens_ref, near_tokens_ref, sems.at[2])
+    fetch.start()
     tok_rows, width = tokens_ref.shape
     chunks = tok_rows // LANES
     devices = back_ref.shape[0]
@@ -168,7 +167,9 @@
         copy = pltpu.make_async_copy(near_ref.at[at, :], quant_ref.at[at, :], sems.at[half])
         copy.start()
         copies.append(copy)
-        diff = tokens_ref[at, :].astype(F32) - quant
+        if half == 0:
+            fetch.wait()
+        diff = near_tokens_ref[at, :].astype(F32) - quant
         loss = jnp.sum(diff * diff, axis=1, keepdims=True) / width
         for i, k in enumerate(near):
             losses = jnp.where(lane == k, loss[i * LANES : (i + 1) * LANES, :], losses)
@@ -228,18 +229,16 @@
     shape = jax.ShapeDtypeStruct
 
     tiles = max(per_dev // LANES, 1)
-    pay, slot, near_tokens = pl.pallas_call(
+    pay, slot = pl.pallas_call(
         functools.partial(request_kernel, devices=devices, per_dev=per_dev, slots=slots),
         out_shape=(
             shape((devices * tiles, LANES), F32),
             shape((-(-chunks // 8) * 8, LANES), F32),
-            shape(tokens.shape, BF16),
         ),
-        in_specs=[VMEM, ANY],
-        out_specs=(VMEM,) * 3,
-        scratch_shapes=[pltpu.SemaphoreType.DMA],
+        in_specs=[VMEM],
+        out_specs=(VMEM,) * 2,
         name="request",
-    )(codes.reshape(chunks, LANES), tokens)
+    )(codes.reshape(chunks, LANES))
     pay_in = lax.all_to_all(pay.reshape(devices, tiles, LANES), AXES, 0, 0)
     pay_in = pay_in.reshape(devices * tiles, LANES)
     send, rank, counts, ent, least = pl.pallas_call(
@@ -258,7 +257,7 @@
     )(pay_in, codebook)
     code_counts = counts.reshape(per_dev)
 
-    def exchange_slots(tokens, near_tokens, codebook, codes, slot, send, rank, ent):
+    def exchange_slots(tokens, codebook, codes, slot, send, rank, ent):
         recv = lax.all_to_all(send, AXES, 0, 0, tiled=True)
         quantized, loss, back = pl.pallas_call(
             functools.partial(loss_kernel, slots=slots, block=min(n_slots, 1024)),
@@ -267,14 +266,15 @@
                 shape((chunks, LANES), F32),
                 shape((devices, LANES), F32),
             ),
-            in_specs=[VMEM] * 4,
+            in_specs=[VMEM, ANY, VMEM, VMEM],
             out_specs=(ANY, VMEM, VMEM),
             scratch_shapes=[
                 pltpu.VMEM((tok_rows, width), BF16),
-                pltpu.SemaphoreType.DMA((2,)),
+                pltpu.VMEM((tok_rows, width), BF16),
+                pltpu.SemaphoreType.DMA((3,)),
             ],
             name="losses",
-        )(slot, near_tokens, recv, ent)
+        )(slot, tokens, recv, ent)
         back_in = lax.all_to_all(back, AXES, 0, 0, tiled=True)
         code_loss, commit, perp = pl.pallas_call(
             functools.partial(collect_kernel, slots=slots, total_tokens=total_tokens),
@@ -291,7 +291,7 @@
             perp.reshape(()),
         )
 
-    def exchange_book(tokens, near_tokens, codebook, codes, slot, send, rank, ent):
+    def exchange_book(tokens, codebook, codes, slot, send, rank, ent):
         spread = jnp.broadcast_to(codebook[None], (devices, per_dev, width))
         book = lax.all_to_all(spread, AXES, 0, 0, tiled=True)
         book = book.reshape(devices * per_dev, width)
@@ -315,7 +315,7 @@
         least[0, 0] < 0.0,
         exchange_book,
         exchange_slots,
-        tokens, near_tokens, codebook, codes, slot, send, rank, ent,
+        tokens, codebook, codes, slot, send, rank, ent,
     )
     return (quantized, token_loss, code_counts, code_loss, commitment, perplexity)
 

time: 55.1 us -> 55.3 us (level)
    pallas_call x1, Pallas kernels: 3.16 us -> 3.94 us  [exchange_slots(): pl.pallas_call(functools.partial(loss_kernel, slots=slots, block=min(n_sl...]
where the time goes in v4:
time: 55.3 us; the launch traced here: 54.9 us
  blocking collectives  43 us (78%)
  Pallas kernels  9.96 us (18%)
  between operations  1.29 us (2%)
  local copies, waits for them, and re-layouts  0.58 us (1%)
    all_to_all x1, blocking collectives, exchange_slots(): recv = lax.all_to_all(send, AXES, 0, 0, tiled=True)  18 us
    all_to_all x1, blocking collectives, on_device(): pay_in = lax.all_to_all(pay.reshape(devices, tiles, LANES), AXES, 0, 0)  14.8 us
    all_to_all x1, blocking collectives, exchange_slots(): back_in = lax.all_to_all(back, AXES, 0, 0, tiled=True)  10.2 us
    pallas_call x1, Pallas kernels, exchange_slots(): pl.pallas_call(functools.partial(loss_kernel, slots=slots, block=min(n_sl...  3.94 us
    pallas_call x1, Pallas kernels, on_device(): pl.pallas_call(functools.partial(serve_kernel, slots=slots, total_tokens=...  2.69 us
    pallas_call x1, Pallas kernels, on_device(): pl.pallas_call(functools.partial(request_kernel, devices=devices, per_dev...  1.79 us
    pallas_call x1, Pallas kernels, exchange_slots(): pl.pallas_call(functools.partial(collect_kernel, slots=slots, total_token...  1.53 us

profile of v4, /device:TPU:0, one launch (start us, length us, event | category | flops | bytes accessed | tf_op | source)
XLA Modules:
  0.0 54.9 jit_solution(7367564960962622203)
XLA Ops:
  0.6 1.8 %request.1 = (f32[128,128]{1,0:T(8,128)}, f32[8,128]{1,0:T(8,128)S(1)}) custom-call(s32[6,128]{1,0:T(8,128)} %bitcast.28), custom_call_target="tpu_custom_call" | custom-call | tf_op jit(solution)/shard_map/request/pallas_call | solution.py:232
  2.4 14.8 %all_to_all.39 = f32[32,4,128]{2,1,0:T(4,128)} all-to-all(f32[32,4,128]{2,1,0:T(4,128)} %bitcast.25), channel_id=1, replica_groups=mesh['row'=4,'col'=8] {'row','col'}, dimensions={0} | all-to-all | bytes 131072 | tf_op jit(solution)/shard_map/all_to_all | solution.py:242
  17.3 2.7 %serve.1 = (bf16[1024,256]{1,0:T(8,128)(2,1)S(1)}, f32[128,128]{1,0:T(8,128)S(1)}, s32[4,128]{1,0:T(4,128)}, f32[1,128]{1,0:T(1,128)S(1)}, f32[1,1]{1,0:T(1,128)}) custom-call(f32[128,128]{1,0:T(8,128)} %bitcast.23, bf16[512,256]{1,0:T(8,128)(2,1)} %book_ref.1), custom_call_target="tpu_custom_call" | custom-call | tf_op jit(solution)/shard_map/serve/pallas_call | solution.py:244
  20.6 33.7 %conditional.1 = (bf16[768,256]{1,0:T(8,128)(2,1)}, f32[768]{0:T(1024)}, f32[512]{0:T(512)S(1)}, f32[]{:T(128)}, f32[]{:T(128)}) conditional(s32[]{:T(128)} %bitcast.19, (bf16[1024,256]{1,0:T(8,128)(2,1)S(1)}, f32[8,128]{1,0:T(8,128)S(1)}, bf16[768,256]{1,0:T(8,128)(2,1)}, f32[1,128]{1,0:T(1,128)S(1)}, f32[128,128]{1,0:T(8,128)S(1)}) %tuple.16, ...), branch_computations={%region_0.0_spmd, %region_1.7_spmd} | conditional | flops 1009665 | bytes 37407740 | solution.py:314
  20.6 18.0 %all_to_all.37 = bf16[32,32,256]{2,1,0:T(8,128)(2,1)} all-to-all(bf16[32,32,256]{2,1,0:T(8,128)(2,1)S(1)} %bitcast.22), channel_id=1, replica_groups=mesh['row'=4,'col'=8] {'row','col'}, dimensions={0} | all-to-all | bytes 1048576 | tf_op jit(solution)/shard_map/cond/branch_0_fun/all_to_all | solution.py:261
  38.6 3.9 %losses.1 = (bf16[768,256]{1,0:T(8,128)(2,1)}, f32[6,128]{1,0:T(8,128)}, f32[32,128]{1,0:T(8,128)}) custom-call(f32[8,128]{1,0:T(8,128)S(1)} %get-tuple-element.18.slot_ref, bf16[768,256]{1,0:T(8,128)(2,1)} %get-tuple-element.19.tokens_ref, bf16[1024,256]{1,0:T(8,128)(2,1)} %bitcast.21, f32[1,128]{1,0:T(1,128)S(1)} %get-tuple-element.21.ent_ref), custom_call_target="tpu_custom_call" | custom-call | tf_op jit(solution)/shard_map/cond/branch_0_fun/losses/pallas_call | solution.py:262
  42.6 10.2 %all_to_all.38 = f32[32,1,128]{2,1,0:T(1,128)} all-to-all(f32[32,1,128]{2,1,0:T(1,128)} %bitcast.27), channel_id=1, replica_groups=mesh['row'=4,'col'=8] {'row','col'}, dimensions={0} | all-to-all | bytes 32768 | tf_op jit(solution)/shard_map/cond/branch_0_fun/all_to_all | solution.py:278
  52.8 1.5 %collect.1 = (f32[4,128]{1,0:T(4,128)S(1)}, f32[1,1]{1,0:T(1,128)}, f32[1,1]{1,0:T(1,128)}) custom-call(f32[32,128]{1,0:T(8,128)} %bitcast.24, f32[128,128]{1,0:T(8,128)S(1)} %get-tuple-element.25.rank_ref), custom_call_target="tpu_custom_call" | custom-call | tf_op jit(solution)/shard_map/cond/branch_0_fun/collect/pallas_call | solution.py:279
  54.3 0.0 copy-start.2
  54.3 0.6 %copy-done.2 = f32[512]{0:T(512)} copy-done((f32[512]{0:T(512)}, f32[512]{0:T(512)S(1)}, u32[]{:S(2)}) %copy-start.2) | copy-done | bytes 2072
Async XLA Ops:
  54.3 0.6 %copy-start.2 = (f32[512]{0:T(512)}, f32[512]{0:T(512)S(1)}, u32[]{:S(2)}) copy-start(f32[512]{0:T(512)S(1)} %get-tuple-element.48) | copy-start | bytes 6148
